TPU v7x, 32 devices: a whole 2x2x4 slice. The times are simulated.
32 devices in a mesh: shell: 2 (over x), pix: 16 (over z, y, core).
Axes of the slice: x: 2, y: 2, z: 4, core: 2. Of those that a mesh axis runs over, the one named last changes fastest.
Arguments:
- block_tile: int32 [4, 1024], P('shell'), may hold values from 0 to 2047, as said below
- cell_index: int32 [4, 1024, 512], P('shell', 'pix'), may hold values from 0 to 2047
- masses: bfloat16 [4, 1024, 512], P('shell', 'pix'), may hold values from 0.125 to 8, as said below
- plane_coef: float32 [4], P('shell'), may hold values from 0.1 to 0.4
- plane_dist: float32 [4], P('shell'), may hold values from 0.2 to 1
- source_inv: float32 [4], P('shell'), may hold values from 0.5 to 1
Outputs:
- convergence: float32 [4, 2048, 2048], P('shell', 'pix')
- shear_one: float32 [4, 2048, 2048], P('shell', 'pix')
- shear_two: float32 [4, 2048, 2048], P('shell', 'pix')
Inputs may be any that keep to these rules, and one draw needn't show every extreme that they name: `block_tile`: each row is 16 aligned runs of 64 entries, one run per index of pix. The entries of a run are distinct, and at most 8 of them lie in one index's rows of tiles (tile b lies in the rows of index b // 128). In every plane some index receives exactly 8 tiles from every run. `masses`: positive particle weights.
All inputs are finite; a program needn't handle non-finite values.
Results may differ from a plain program's by a relative error of at most 0.0003.
Values sent between devices are 32-bit elements; how exact they have to be, the bound alone decides.
A program may use at most 64 MiB of HBM per device.

v0:
```python
from functools import partial
import math
import jax
import jax.numpy as jnp
from jax import lax
from jax.sharding import PartitionSpec as P

L = 2048
TR = 16
TC = 128
HIGHEST = lax.Precision.HIGHEST


def entering(value, axis, join, neutral):
    count, mine = (lax.axis_size(axis), lax.axis_index(axis))
    pieces = jax.tree.map(lambda part: lax.all_gather(part, axis), value)
    running = jax.tree.map(
        lambda part, zero: jnp.full_like(part, 0) + jnp.asarray(zero, part.dtype), value, neutral
    )

    def lap(position, running):
        longer = join(running, jax.tree.map(lambda part: part[position], pieces))
        return jax.tree.map(lambda new, old: jnp.where(position < mine, new, old), longer, running)

    return lax.fori_loop(0, count - 1, lap, running)


def dft_table(left_size, right_size, period, sign_value):
    left_idx = jnp.arange(left_size)[:, None]
    right_idx = jnp.arange(right_size)[None, :]
    angle = 2.0 * math.pi / period * (left_idx * right_idx % period).astype(jnp.float32)
    return (jnp.cos(angle), sign_value * jnp.sin(angle))


def mix_outer(table, real_part, imag_part):
    cosine, sine_part = table
    contract = partial(jnp.einsum, "ab,...bc->...ac", precision=HIGHEST)
    return (
        contract(cosine, real_part) - contract(sine_part, imag_part),
        contract(sine_part, real_part) + contract(cosine, imag_part),
    )


def mix_inner(table, real_part, imag_part):
    cosine, sine_part = table
    product = partial(jnp.matmul, precision=HIGHEST)
    return (
        product(real_part, cosine) - product(imag_part, sine_part),
        product(real_part, sine_part) + product(imag_part, cosine),
    )


def twist(table, real_part, imag_part):
    cosine, sine_part = table
    return (real_part * cosine - imag_part * sine_part, real_part * sine_part + imag_part * cosine)


def transform_last(real_part, imag_part, sign_value):
    length = real_part.shape[-1]
    inner = math.gcd(length, 128)
    outer = length // inner
    leading = real_part.shape[:-1]
    real_part = real_part.reshape(leading + (outer, inner))
    imag_part = imag_part.reshape(leading + (outer, inner))
    outer_table = dft_table(outer, outer, outer, sign_value)
    inner_table = dft_table(inner, inner, inner, sign_value)
    twiddle = dft_table(outer, inner, length, sign_value)
    if sign_value < 0:
        real_part, imag_part = mix_outer(outer_table, real_part, imag_part)
        real_part, imag_part = twist(twiddle, real_part, imag_part)
        real_part, imag_part = mix_inner(inner_table, real_part, imag_part)
    else:
        real_part, imag_part = mix_inner(inner_table, real_part, imag_part)
        real_part, imag_part = twist(twiddle, real_part, imag_part)
        real_part, imag_part = mix_outer(outer_table, real_part, imag_part)
    return (real_part.reshape(leading + (length,)), imag_part.reshape(leading + (length,)))


def frequency_of(position, length):
    inner = math.gcd(length, 128)
    outer = length // inner
    frequency = position // inner + outer * (position % inner)
    signed = jnp.where(frequency >= length // 2, frequency - length, frequency).astype(jnp.float32)
    keep_mask = (frequency != length // 2).astype(jnp.float32)
    return (signed, keep_mask)


def add_pairs(earlier_pair, later_pair):
    return (earlier_pair[0] + later_pair[0], earlier_pair[1] + later_pair[1])


def deposit_group(item):
    cell_ids, weights = item
    tile_rows = cell_ids // TC
    tile_cols = cell_ids % TC
    row_hot = jnp.where(
        tile_rows[:, None, :] == jnp.arange(TR)[None, :, None],
        weights[:, None, :],
        jnp.zeros((), jnp.bfloat16),
    )
    col_hot = (tile_cols[:, :, None] == jnp.arange(TC)[None, None, :]).astype(jnp.bfloat16)
    return jnp.einsum("grk,gkc->grc", row_hot, col_hot, preferred_element_type=jnp.float32)


def rows_to_sending(packed, groups, slab, cols_own):
    count, fields = (packed.shape[0], packed.shape[1])
    return (
        packed.reshape(count, fields, slab, groups, cols_own)
        .transpose(3, 0, 1, 4, 2)
        .reshape(groups, count, fields, cols_own * slab)
    )


def arrived_to_columns(arrived, groups, slab, cols_own):
    count, fields = (arrived.shape[1], arrived.shape[2])
    return (
        arrived.reshape(groups, count, fields, cols_own, slab)
        .transpose(1, 2, 3, 0, 4)
        .reshape(count, fields, cols_own, groups * slab)
    )


def columns_to_sending(stacked, groups, slab, cols_own):
    count, fields = (stacked.shape[0], stacked.shape[1])
    return (
        stacked.reshape(count, fields, cols_own, groups, slab)
        .transpose(3, 0, 1, 2, 4)
        .reshape(groups, count, fields, cols_own * slab)
    )


def landed_to_rows(landed, groups, slab, cols_own):
    count, fields = (landed.shape[1], landed.shape[2])
    return (
        landed.reshape(groups, count, fields, cols_own, slab)
        .transpose(1, 2, 4, 0, 3)
        .reshape(count, fields, slab, groups * cols_own)
    )


def local(block_tile, cell_index, masses, plane_coef, plane_dist, source_inv):
    groups = lax.axis_size("pix")
    my_index = lax.axis_index("pix")
    planes, local_tiles, per_tile = cell_index.shape
    slab = L // groups
    per_owner = slab // TR * (L // TC)
    cap = max(1, 2 * local_tiles // groups)
    flat = TR * TC
    batch_tiles = 8
    deposited = lax.map(
        deposit_group,
        (cell_index.reshape(-1, batch_tiles, per_tile), masses.reshape(-1, batch_tiles, per_tile)),
    )
    tile_sums = deposited.reshape(planes, local_tiles, flat)
    table = block_tile.reshape(planes, groups, local_tiles)
    owner = table // per_owner
    earlier = jnp.arange(local_tiles)[:, None] < jnp.arange(local_tiles)[None, :]
    same_owner = owner[:, :, :, None] == owner[:, :, None, :]
    rank = jnp.sum(jnp.where(same_owner & earlier[None, None], 1, 0), axis=2)
    slot = owner * cap + rank
    my_slots = lax.dynamic_index_in_dim(slot, my_index, axis=1, keepdims=False)
    slot_grid = jnp.arange(groups)[:, None] * cap + jnp.arange(cap)[None, :]
    send_hot = (my_slots[:, None, None, :] == slot_grid[None, :, :, None]).astype(jnp.float32)
    outgoing = jnp.einsum("pnct,ptf->npcf", send_hot, tile_sums, precision=HIGHEST)
    incoming = lax.all_to_all(outgoing, "pix", split_axis=0, concat_axis=0, tiled=True)
    local_index = table - my_index * per_owner
    is_mine = owner == my_index
    tile_hot = (is_mine[..., None] & (local_index[..., None] == jnp.arange(per_owner))).astype(
        jnp.float32
    )
    slot_hot = (rank[..., None] == jnp.arange(cap)).astype(jnp.float32)
    placing = jnp.einsum("pstl,pstc->plsc", tile_hot, slot_hot, precision=HIGHEST)
    slab_tiles = jnp.einsum("plsc,spcf->plf", placing, incoming, precision=HIGHEST)
    density = (
        slab_tiles.reshape(planes, slab // TR, L // TC, TR, TC)
        .transpose(0, 1, 3, 2, 4)
        .reshape(planes, slab, L)
    )
    total = lax.psum(jnp.sum(density, axis=(1, 2)), "pix")
    contrast = density / (total / (L * L))[:, None, None] - 1.0
    near_local = jnp.cumsum(plane_coef[:, None, None] * contrast, axis=0)
    far_local = jnp.cumsum((plane_coef * plane_dist)[:, None, None] * contrast, axis=0)
    blank = jnp.zeros((slab, L), jnp.float32)
    near_before, far_before = entering(
        (near_local[-1], far_local[-1]), "shell", add_pairs, (blank, blank)
    )
    convergence = near_before + near_local - source_inv[:, None, None] * (far_before + far_local)
    cols_own = L // groups
    wave_x, keep_x = frequency_of(my_index * cols_own + jnp.arange(cols_own), L)
    wave_y, keep_y = frequency_of(jnp.arange(L), L)
    wave_x = wave_x[:, None]
    wave_y = wave_y[None, :]
    both_keep = keep_x[:, None] * keep_y[None, :]
    wave_power = jnp.maximum(wave_x * wave_x + wave_y * wave_y, 1.0)
    kernel_one = both_keep * (wave_x * wave_x - wave_y * wave_y) / wave_power
    kernel_two = both_keep * 2.0 * wave_x * wave_y / wave_power
    scale = 1.0 / (L * L)
    spec_real, spec_imag = transform_last(convergence[0::2], convergence[1::2], -1.0)
    sending = rows_to_sending(jnp.stack([spec_real, spec_imag], axis=1), groups, slab, cols_own)
    arrived = lax.all_to_all(sending, "pix", split_axis=0, concat_axis=0, tiled=True)
    columns = arrived_to_columns(arrived, groups, slab, cols_own)
    row_real, row_imag = transform_last(columns[:, 0], columns[:, 1], -1.0)
    first_real, first_imag = transform_last(row_real * kernel_one, row_imag * kernel_one, 1.0)
    second_real, second_imag = transform_last(row_real * kernel_two, row_imag * kernel_two, 1.0)
    stacked = jnp.stack([first_real, first_imag, second_real, second_imag], axis=1)
    landed = lax.all_to_all(
        columns_to_sending(stacked, groups, slab, cols_own),
        "pix",
        split_axis=0,
        concat_axis=0,
        tiled=True,
    )
    row_layout = landed_to_rows(landed, groups, slab, cols_own)
    even_one, odd_one = transform_last(row_layout[:, 0], row_layout[:, 1], 1.0)
    even_two, odd_two = transform_last(row_layout[:, 2], row_layout[:, 3], 1.0)
    shear_one = jnp.stack([even_one, odd_one], axis=1).reshape(planes, slab, L)
    shear_two = jnp.stack([even_two, odd_two], axis=1).reshape(planes, slab, L)
    return (convergence, shear_one * scale, shear_two * scale)


def solution(mesh):
    placed = (
        P("shell", None),
        P("shell", "pix", None),
        P("shell", "pix", None),
        P("shell"),
        P("shell"),
        P("shell"),
    )
    return jax.shard_map(
        local,
        mesh=mesh,
        in_specs=placed,
        out_specs=(P("shell", "pix", None), P("shell", "pix", None), P("shell", "pix", None)),
        check_vma=False,
    )
```

profile of v0, /device:TPU:1, one launch (start us, length us, event | category | flops | bytes accessed | tf_op | source)
XLA Modules:
  0.0 498.4 jit_solution(13083244063688740668)
XLA Ops:
  8.0 56.0 %while.8 = (s32[]{:T(128)}, f32[16,8,16,128]{3,2,1,0:T(8,128)S(1)}, s32[16,8,512]{2,1,0:T(8,128)}, bf16[16,8,512]{2,1,0:T(8,128)(2,1)}, s32[]{:T(128)}) while((s32[]{:T(128)}, f32[16,8,16,128]{3,2,1,0:T(8,128)S(1)}, s32[16,8,512]{2,1,0:T(8,128)}, bf16[16,8,512]{2,1,0:T(8,128)(2,1)}, s32[]{:T(128)}) %tuple.63), condition=%wide.region_2.3_spmd, body=%wide.region_1.2_spmd.sunk | while | flops 17534976 | bytes 196693 | solution.py:150
  65.7 2.5 copy.183
  68.2 7.3 %all-to-all-start = ((f32[16,2,8,2048]{3,2,1,0:T(8,128)}), f32[16,2,8,2048]{3,2,1,0:T(8,128)S(1)}, u32[]{:S(2)}, u32[]{:S(2)}) async-start(f32[16,2,8,2048]{3,2,1,0:T(8,128)} %copy.183), calls=%async_computation | async-start | bytes 4194304 | tf_op jit(solution)/shard_map/all_to_all | solution.py:165
  76.9 40.2 %all-to-all-done = f32[16,2,8,2048]{3,2,1,0:T(8,128)S(1)} async-done(((f32[16,2,8,2048]{3,2,1,0:T(8,128)}), f32[16,2,8,2048]{3,2,1,0:T(8,128)S(1)}, u32[]{:S(2)}, u32[]{:S(2)}) %all-to-all-start) | async-done | bytes 2097184 | tf_op jit(solution)/shard_map/all_to_all | solution.py:165
  117.1 3.2 bitcast_reduce_fusion
  120.3 33.9 %psum.7 = f32[2]{0:T(128)S(1)} all-reduce(f32[2]{0:T(128)S(1)} %get-tuple-element.117), channel_id=1, replica_groups=mesh['shell'=2,'pix'=16] {'pix'}, use_global_device_ids=true, to_apply=%region_4.5 | all-reduce | flops 2 | bytes 16 | tf_op jit(solution)/shard_map/psum | solution.py:179
  154.2 2.0 copy.236
  156.2 2.0 copy.185
  158.2 1.7 reshape.931
  165.7 31.5 %all-gather.3.cloned.1.call-done = f32[2,128,2048]{2,1,0:T(8,128)} async-done(((f32[1,128,2048]{2,1,0:T(8,128)}), f32[2,128,2048]{2,1,0:T(8,128)}) %all-gather.3.cloned.1.call-update) | async-done | bytes 2097168 | tf_op jit(solution)/shard_map/all_gather | solution.py:16
  198.6 33.9 %all-gather.5.cloned.1.call-done = f32[2,128,2048]{2,1,0:T(8,128)} async-done(((f32[1,128,2048]{2,1,0:T(8,128)}), f32[2,128,2048]{2,1,0:T(8,128)}) %all-gather.5.cloned.1.call-update) | async-done | bytes 2097168 | tf_op jit(solution)/shard_map/all_gather | solution.py:16
  245.7 2.0 fusion.31
  247.9 1.8 copy.190
  249.7 6.4 %all-to-all-start.1 = ((f32[16,1,2,16384]{3,1,2,0:T(1,128)}), f32[16,1,2,16384]{3,1,2,0:T(1,128)S(1)}, u32[]{:S(2)}, u32[]{:S(2)}) async-start(f32[16,1,2,16384]{3,1,2,0:T(1,128)} %bitcast.319), calls=%async_computation.1 | async-start | bytes 4194304 | tf_op jit(solution)/shard_map/all_to_all | solution.py:200
  256.2 41.4 %all-to-all-done.1 = f32[16,1,2,16384]{3,1,2,0:T(1,128)S(1)} async-done(((f32[16,1,2,16384]{3,1,2,0:T(1,128)}), f32[16,1,2,16384]{3,1,2,0:T(1,128)S(1)}, u32[]{:S(2)}, u32[]{:S(2)}) %all-to-all-start.1) | async-done | bytes 2097184 | tf_op jit(solution)/shard_map/all_to_all | solution.py:200
  297.6 1.8 copy.191
  299.4 2.6 fusion.465
  304.7 1.7 copy.235
  314.4 1.6 fusion.97
  324.5 1.9 multiply_add_fusion.3
  326.4 2.0 fusion.65
  328.4 1.6 fusion.67
  330.0 1.6 fusion.59
  331.6 1.6 fusion.61
  333.3 1.6 fusion.28
  334.9 1.6 fusion.27
  336.6 1.6 fusion.26
  338.2 1.8 fusion.25
  341.7 103.1 %all_to_all.15 = f32[16,1,4,16384]{3,1,2,0:T(1,128)S(1)} all-to-all(f32[16,1,4,16384]{3,1,2,0:T(1,128)S(1)} %bitcast.304), channel_id=1, replica_groups=mesh['shell'=2,'pix'=16] {'pix'}, dimensions={0} | all-to-all | bytes 8388608 | tf_op jit(solution)/shard_map/all_to_all | solution.py:206
  445.6 1.9 fusion.91
  447.6 1.9 fusion.108
  449.5 1.9 fusion.94
  451.4 1.9 fusion.111
  453.4 2.0 convolution_subtract_fusion.3
  455.4 2.2 convolution_add_fusion.3
  457.5 2.0 convolution_subtract_fusion.1
  459.5 2.3 multiply_add_fusion
  461.8 1.6 fusion.47
  463.4 1.6 fusion.49
  465.1 1.6 fusion.53
  466.7 1.6 fusion.55
  468.3 2.8 fusion.22
  471.2 2.6 fusion.21
  473.8 2.4 stack_reshape.21
  476.2 2.4 stack_reshape.20
  478.5 2.6 fusion.24
  481.1 2.6 fusion.23
  483.7 2.5 stack_reshape.9
  (154 shorter events, 106.5 us)
Async XLA Ops:
  68.2 48.9 %all-to-all-start = ((f32[16,2,8,2048]{3,2,1,0:T(8,128)}), f32[16,2,8,2048]{3,2,1,0:T(8,128)S(1)}, u32[]{:S(2)}, u32[]{:S(2)}) async-start(f32[16,2,8,2048]{3,2,1,0:T(8,128)} %copy.183), calls=%async_computation | async-start | bytes 4194304 | tf_op jit(solution)/shard_map/all_to_all | solution.py:165
  75.6 121.7 %all-gather.3.cloned.1.call-start = ((), (), s32[]{:S(2)}) async-start(), calls=%async_computation.3 | async-start | bytes 3145728 | tf_op jit(solution)/shard_map/all_gather | solution.py:16
  158.2 1.7 copy-start.10
  160.2 1.3 copy-start
  161.6 1.4 copy-start.12
  162.7 69.9 %all-gather.5.cloned.1.call-start = ((), (), s32[]{:S(2)}) async-start(), calls=%async_computation.4 | async-start | bytes 3145728 | tf_op jit(solution)/shard_map/all_gather | solution.py:16
  163.3 1.3 copy-start.2
  165.7 68.3 %copy-start.1 = (f32[2,128,2048]{2,1,0:T(8,128)S(1)}, f32[2,128,2048]{2,1,0:T(8,128)}, u32[]{:S(2)}) copy-start(f32[2,128,2048]{2,1,0:T(8,128)} %copy-done) | copy-start | bytes 6291460
  165.7 68.3 %copy-start.11 = (f32[2]{0:T(128)S(1)}, f32[2]{0:T(128)}, u32[]{:S(2)}) copy-start(f32[2]{0:T(128)} %param.13) | copy-start | bytes 28
  232.5 1.9 copy-start.3
  235.1 1.3 copy-start.4
  249.7 47.9 %all-to-all-start.1 = ((f32[16,1,2,16384]{3,1,2,0:T(1,128)}), f32[16,1,2,16384]{3,1,2,0:T(1,128)S(1)}, u32[]{:S(2)}, u32[]{:S(2)}) async-start(f32[16,1,2,16384]{3,1,2,0:T(1,128)} %bitcast.319), calls=%async_computation.1 | async-start | bytes 4194304 | tf_op jit(solution)/shard_map/all_to_all | solution.py:200
  481.1 5.1 %copy-start.5 = (f32[1,128,16,128]{3,2,1,0:T(8,128)S(1)}, f32[1,128,16,128]{3,2,1,0:T(8,128)}, u32[]{:S(2)}) copy-start(f32[1,128,16,128]{3,2,1,0:T(8,128)} %fusion.24) | copy-start | bytes 3145732
  483.7 3.7 copy-start.6
  483.7 3.7 copy-start.7
  487.4 1.5 copy-start.8
  487.4 2.3 copy-start.9
Sparse Core Ops, SparseCore 0:
  162.8 34.4 all-gather.2
  199.4 33.0 all-gather.4
where the time goes:
time: 508 us; the launch traced here: 498 us
  waiting for transfers between devices  147 us (29%)
  blocking collectives  137 us (27%)
  matrix products  106 us (21%)
  local copies, waits for them, and re-layouts  47.2 us (9%)
  other arithmetic  31.7 us (6%)
  between operations  15.1 us (3%)
  starting transfers between devices  14 us (3%)
    all_to_all x1, blocking collectives, local(): lax.all_to_all(columns_to_sending(stacked, groups, slab, cols_own), 'pix'...  103 us
    all_gather x2, waiting for transfers between devices, entering(): pieces = jax.tree.map(lambda part: lax.all_gather(part, axis), value)  65.5 us
    all_to_all x1, waiting for transfers between devices, local(): lax.all_to_all(sending, 'pix', split_axis=0, concat_axis=0, tiled=True)  41.4 us
    all_to_all x1, waiting for transfers between devices, local(): lax.all_to_all(outgoing, 'pix', split_axis=0, concat_axis=0, tiled=True)  40.2 us
    psum x1, blocking collectives, local(): total = lax.psum(jnp.sum(density, axis=(1, 2)), 'pix')  33.9 us
    dot_general x16, matrix products, deposit_group(): jnp.einsum('grk,gkc->grc', row_hot, col_hot, preferred_element_type=jnp.f...  21.1 us
    select_n x16, other arithmetic, deposit_group(): tile_cols = cell_ids % TC  11.7 us
    select_n x16, other arithmetic, deposit_group(): tile_rows = cell_ids // TC  11.7 us
  transfers between devices with their start and end apart: 4, of which 4 were waited for; matrix products, arithmetic and copies ran while one was open for 1% of the time, Pallas kernels for 0%

commit v1 on v0

--- a/solution.py
+++ b/solution.py
@@ -197,7 +197,15 @@
     scale = 1.0 / (L * L)
     spec_real, spec_imag = transform_last(convergence[0::2], convergence[1::2], -1.0)
     sending = rows_to_sending(jnp.stack([spec_real, spec_imag], axis=1), groups, slab, cols_own)
-    arrived = lax.all_to_all(sending, "pix", split_axis=0, concat_axis=0, tiled=True)
+    ways, here = (lax.axis_size("pix"), lax.axis_index("pix"))
+    width = sending.shape[0] // ways
+    turned = jnp.roll(sending, -here * width, axis=0)
+    got = [lax.slice_in_dim(turned, 0, width, axis=0)]
+    for far in range(1, ways):
+        sent = lax.slice_in_dim(turned, far * width, (far + 1) * width, axis=0)
+        got.append(lax.ppermute(sent, "pix", [(d, (d + far) % ways) for d in range(ways)]))
+    line = jnp.concatenate(got[::-1], axis=0)
+    arrived = jnp.roll(line, (here + 1) * got[0].shape[0], axis=0)
     columns = arrived_to_columns(arrived, groups, slab, cols_own)
     row_real, row_imag = transform_last(columns[:, 0], columns[:, 1], -1.0)
     first_real, first_imag = transform_last(row_real * kernel_one, row_imag * kernel_one, 1.0)

time: 508 us -> 549 us (1.081)
  starting transfers between devices: 14 us -> 38.6 us
  other arithmetic: 31.7 us -> 47.1 us
  blocking collectives: 137 us -> 131 us
    ppermute x0 -> x15, waiting for transfers between devices: none -> 47.9 us  [local(): lax.ppermute(sent, 'pix', [(d, (d + far) % ways) for d in range(ways)])]
    all_to_all x1 -> x0, waiting for transfers between devices: 41.4 us -> none  [local(): lax.all_to_all(sending, 'pix', split_axis=0, concat_axis=0, tiled=True)]
    ppermute x0 -> x15, starting transfers between devices: none -> 30.9 us  [local(): lax.ppermute(sent, 'pix', [(d, (d + far) % ways) for d in range(ways)])]
    concatenate x0 -> x2, other arithmetic: none -> 12.5 us  [the longest x1 6.67 us: local(): turned = jnp.roll(sending, -here * width, axis=0)]
    all_to_all x1 -> x0, starting transfers between devices: 6.38 us -> none  [local(): lax.all_to_all(sending, 'pix', split_axis=0, concat_axis=0, tiled=True)]
    all_to_all x1, blocking collectives: 103 us -> 97.5 us  [local(): lax.all_to_all(columns_to_sending(stacked, groups, slab, cols_own), 'pix'...]
  transfers between devices with their start and end apart: 4 -> 18, of which waited for: 4 -> 13; matrix products, arithmetic and copies ran while one was open for 1% -> 2% of each run, Pallas kernels for 0% -> 0%
where the time goes in v1:
time: 549 us; the launch traced here: 539 us
  waiting for transfers between devices  152 us (28%)
  blocking collectives  131 us (24%)
  matrix products  106 us (19%)
  local copies, waits for them, and re-layouts  48.1 us (9%)
  other arithmetic  47.1 us (9%)
  starting transfers between devices  38.6 us (7%)
  between operations  15.4 us (3%)
    all_to_all x1, blocking collectives, local(): lax.all_to_all(columns_to_sending(stacked, groups, slab, cols_own), 'pix'...  97.5 us
    all_gather x2, waiting for transfers between devices, entering(): pieces = jax.tree.map(lambda part: lax.all_gather(part, axis), value)  63.7 us
    ppermute x15, waiting for transfers between devices, local(): lax.ppermute(sent, 'pix', [(d, (d + far) % ways) for d in range(ways)])  47.9 us
    all_to_all x1, waiting for transfers between devices, local(): lax.all_to_all(outgoing, 'pix', split_axis=0, concat_axis=0, tiled=True)  40.2 us
    psum x1, blocking collectives, local(): total = lax.psum(jnp.sum(density, axis=(1, 2)), 'pix')  33.9 us
    ppermute x15, starting transfers between devices, local(): lax.ppermute(sent, 'pix', [(d, (d + far) % ways) for d in range(ways)])  30.9 us
    dot_general x16, matrix products, deposit_group(): jnp.einsum('grk,gkc->grc', row_hot, col_hot, preferred_element_type=jnp.f...  21.1 us
    select_n x16, other arithmetic, deposit_group(): tile_cols = cell_ids % TC  11.7 us
  transfers between devices with their start and end apart: 18, of which 13 were waited for; matrix products, arithmetic and copies ran while one was open for 2% of the time, Pallas kernels for 0%

profile of v1, /device:TPU:1, one launch (start us, length us, event | category | flops | bytes accessed | tf_op | source)
XLA Modules:
  0.0 538.8 jit_solution(9536464123188302767)
XLA Ops:
  8.0 56.0 %while.8 = (s32[]{:T(128)}, f32[16,8,16,128]{3,2,1,0:T(8,128)S(1)}, s32[16,8,512]{2,1,0:T(8,128)}, bf16[16,8,512]{2,1,0:T(8,128)(2,1)}, s32[]{:T(128)}) while((s32[]{:T(128)}, f32[16,8,16,128]{3,2,1,0:T(8,128)S(1)}, s32[16,8,512]{2,1,0:T(8,128)}, bf16[16,8,512]{2,1,0:T(8,128)(2,1)}, s32[]{:T(128)}) %tuple.78), condition=%wide.region_2.3_spmd, body=%wide.region_1.2_spmd.sunk | while | flops 17534976 | bytes 196693 | solution.py:150
  65.7 2.5 copy.183
  68.2 7.3 %all-to-all-start = ((f32[16,2,8,2048]{3,2,1,0:T(8,128)}), f32[16,2,8,2048]{3,2,1,0:T(8,128)S(1)}, u32[]{:S(2)}, u32[]{:S(2)}) async-start(f32[16,2,8,2048]{3,2,1,0:T(8,128)} %copy.183), calls=%async_computation | async-start | bytes 4194304 | tf_op jit(solution)/shard_map/all_to_all | solution.py:165
  76.9 40.2 %all-to-all-done = f32[16,2,8,2048]{3,2,1,0:T(8,128)S(1)} async-done(((f32[16,2,8,2048]{3,2,1,0:T(8,128)}), f32[16,2,8,2048]{3,2,1,0:T(8,128)S(1)}, u32[]{:S(2)}, u32[]{:S(2)}) %all-to-all-start) | async-done | bytes 2097184 | tf_op jit(solution)/shard_map/all_to_all | solution.py:165
  117.1 3.2 bitcast_reduce_fusion
  120.3 33.9 %psum.7 = f32[2]{0:T(128)S(1)} all-reduce(f32[2]{0:T(128)S(1)} %get-tuple-element.133), channel_id=1, replica_groups=mesh['shell'=2,'pix'=16] {'pix'}, use_global_device_ids=true, to_apply=%region_4.5 | all-reduce | flops 2 | bytes 16 | tf_op jit(solution)/shard_map/psum | solution.py:179
  154.2 2.0 copy.236
  156.2 2.0 copy.185
  167.5 29.7 %all-gather.3.cloned.1.call-done = f32[2,128,2048]{2,1,0:T(8,128)} async-done(((f32[1,128,2048]{2,1,0:T(8,128)}), f32[2,128,2048]{2,1,0:T(8,128)}) %all-gather.3.cloned.1.call-update) | async-done | bytes 2097168 | tf_op jit(solution)/shard_map/all_gather | solution.py:16
  198.6 33.9 %all-gather.5.cloned.1.call-done = f32[2,128,2048]{2,1,0:T(8,128)} async-done(((f32[1,128,2048]{2,1,0:T(8,128)}), f32[2,128,2048]{2,1,0:T(8,128)}) %all-gather.5.cloned.1.call-update) | async-done | bytes 2097168 | tf_op jit(solution)/shard_map/all_gather | solution.py:16
  245.7 2.0 fusion.33
  249.7 6.7 %fusion.14 = f32[16,1,2,16384]{3,1,2,0:T(1,128)S(1)} fusion(s32[]{:T(128)S(6)} %select_n.400, f32[16,1,2,16384]{3,1,2,0:T(1,128)} %bitcast.320), kind=kLoop, calls=%fused_computation.29 | loop fusion | flops 524288 | bytes 4194308 | tf_op jit(solution)/shard_map/jit(_roll_dynamic)/concatenate | solution.py:202
  260.4 1.9 collective-permute-start.13
  263.7 6.1 %collective-permute-start.1 = (f32[1,1,2,16384]{3,1,2,0:T(1,128)}, f32[1,1,2,16384]{3,1,2,0:T(1,128)S(1)}, u32[]{:S(2)}, u32[]{:S(2)}) collective-permute-start(f32[1,1,2,16384]{3,1,2,0:T(1,128)} %get-tuple-element.125), channel_id=1, source_target_pairs={{0,14},{1,15},{2,0},{3,1},{4,2},{5,3},{6,4},{7,5},{8,6},{9,7},{10,... | collective-permute-start | bytes 393224 | tf_op jit(solution)/shard_map/ppermute | solution.py:206
  272.5 4.1 collective-permute-start.2
  276.7 2.8 collective-permute-done.2
  279.5 2.8 collective-permute-start.3
  282.3 2.3 collective-permute-done.3
  284.6 2.9 collective-permute-start.4
  287.5 3.2 collective-permute-done.4
  290.7 3.9 collective-permute-start.5
  294.6 2.2 collective-permute-done.5
  296.8 3.1 collective-permute-start.6
  300.0 7.3 %collective-permute-done.6 = f32[1,1,2,16384]{3,1,2,0:T(1,128)S(1)} collective-permute-done((f32[1,1,2,16384]{3,1,2,0:T(1,128)S(1)}, f32[1,1,2,16384]{3,1,2,0:T(1,128)S(1)}, u32[]{:S(2)}, u32[]{:S(2)}) %collective-permute-start.6) | collective-permute-done | bytes 131104 | tf_op jit(solution)/shard_map/ppermute | solution.py:206
  308.2 6.6 %collective-permute-done.7 = f32[1,1,2,16384]{3,1,2,0:T(1,128)S(1)} collective-permute-done((f32[1,1,2,16384]{3,1,2,0:T(1,128)S(1)}, f32[1,1,2,16384]{3,1,2,0:T(1,128)S(1)}, u32[]{:S(2)}, u32[]{:S(2)}) %collective-permute-start.7) | collective-permute-done | bytes 131104 | tf_op jit(solution)/shard_map/ppermute | solution.py:206
  314.9 9.6 %collective-permute-done.8 = f32[1,1,2,16384]{3,1,2,0:T(1,128)S(1)} collective-permute-done((f32[1,1,2,16384]{3,1,2,0:T(1,128)S(1)}, f32[1,1,2,16384]{3,1,2,0:T(1,128)S(1)}, u32[]{:S(2)}, u32[]{:S(2)}) %collective-permute-start.8) | collective-permute-done | bytes 131104 | tf_op jit(solution)/shard_map/ppermute | solution.py:206
  325.3 6.3 %collective-permute-done.9 = f32[1,1,2,16384]{3,1,2,0:T(1,128)S(1)} collective-permute-done((f32[1,1,2,16384]{3,1,2,0:T(1,128)S(1)}, f32[1,1,2,16384]{3,1,2,0:T(1,128)S(1)}, u32[]{:S(2)}, u32[]{:S(2)}) %collective-permute-start.9) | collective-permute-done | bytes 131104 | tf_op jit(solution)/shard_map/ppermute | solution.py:206
  332.7 5.7 %collective-permute-done.10 = f32[1,1,2,16384]{3,1,2,0:T(1,128)S(1)} collective-permute-done((f32[1,1,2,16384]{3,1,2,0:T(1,128)S(1)}, f32[1,1,2,16384]{3,1,2,0:T(1,128)S(1)}, u32[]{:S(2)}, u32[]{:S(2)}) %collective-permute-start.10) | collective-permute-done | bytes 131104 | tf_op jit(solution)/shard_map/ppermute | solution.py:206
  338.6 5.8 %fusion.13 = f32[16,1,2,16384]{3,1,2,0:T(1,128)} fusion(s32[]{:T(128)S(6)} %select_n.402, f32[16,1,2,16384]{3,1,2,0:T(1,128)S(1)} %slice_dynamic-update-slice_fusion), kind=kLoop, calls=%fused_computation.28 | loop fusion | flops 524288 | bytes 4194308 | tf_op jit(solution)/shard_map/jit(_roll_dynamic)/concatenate | solution.py:208
  344.5 2.1 copy.191
  370.3 1.9 multiply_add_fusion.3
  372.2 2.1 fusion.67
  387.6 97.5 %all_to_all.10 = f32[16,1,4,16384]{3,1,2,0:T(1,128)S(1)} all-to-all(f32[16,1,4,16384]{3,1,2,0:T(1,128)S(1)} %bitcast.304), channel_id=1, replica_groups=mesh['shell'=2,'pix'=16] {'pix'}, dimensions={0} | all-to-all | bytes 8388608 | tf_op jit(solution)/shard_map/all_to_all | solution.py:214
  485.9 1.9 fusion.93
  487.9 1.9 fusion.110
  489.8 1.9 fusion.96
  491.8 1.9 fusion.113
  493.7 2.0 convolution_subtract_fusion.3
  495.7 2.2 convolution_add_fusion.3
  497.9 2.0 convolution_subtract_fusion.1
  499.8 2.3 multiply_add_fusion
  508.7 2.8 fusion.24
  511.5 2.6 fusion.23
  514.1 2.4 stack_reshape.21
  516.5 2.4 stack_reshape.20
  518.8 2.6 fusion.26
  521.5 2.6 fusion.25
  524.1 2.5 stack_reshape.9
  (215 shorter events, 145.4 us)
Async XLA Ops:
  68.2 48.9 %all-to-all-start = ((f32[16,2,8,2048]{3,2,1,0:T(8,128)}), f32[16,2,8,2048]{3,2,1,0:T(8,128)S(1)}, u32[]{:S(2)}, u32[]{:S(2)}) async-start(f32[16,2,8,2048]{3,2,1,0:T(8,128)} %copy.183), calls=%async_computation | async-start | bytes 4194304 | tf_op jit(solution)/shard_map/all_to_all | solution.py:165
  75.6 121.7 %all-gather.3.cloned.1.call-start = ((), (), s32[]{:S(2)}) async-start(), calls=%async_computation.2 | async-start | bytes 3145728 | tf_op jit(solution)/shard_map/all_gather | solution.py:16
  158.2 1.7 copy-start.14
  160.2 1.3 copy-start
  161.6 1.4 copy-start.18
  162.7 69.9 %all-gather.5.cloned.1.call-start = ((), (), s32[]{:S(2)}) async-start(), calls=%async_computation.3 | async-start | bytes 3145728 | tf_op jit(solution)/shard_map/all_gather | solution.py:16
  163.3 1.3 copy-start.2
  167.5 66.5 %copy-start.1 = (f32[2,128,2048]{2,1,0:T(8,128)S(1)}, f32[2,128,2048]{2,1,0:T(8,128)}, u32[]{:S(2)}) copy-start(f32[2,128,2048]{2,1,0:T(8,128)} %copy-done) | copy-start | bytes 6291460
  167.5 66.5 %copy-start.15 = (f32[2]{0:T(128)S(1)}, f32[2]{0:T(128)}, u32[]{:S(2)}) copy-start(f32[2]{0:T(128)} %param.15) | copy-start | bytes 28
  232.5 1.9 copy-start.3
  235.1 1.3 copy-start.4
  257.3 6.4 %collective-permute-start = (f32[1,1,2,16384]{3,1,2,0:T(1,128)}, f32[1,1,2,16384]{3,1,2,0:T(1,128)}, u32[]{:S(2)}, u32[]{:S(2)}) collective-permute-start(f32[1,1,2,16384]{3,1,2,0:T(1,128)} %get-tuple-element.126), channel_id=1, source_target_pairs={{0,15},{1,0},{2,1},{3,2},{4,3},{5,4},{6,5},{7,6},{8,7},{9,8},{10,9... | collective-permute-start | bytes 393224 | tf_op jit(solution)/shard_map/ppermute | solution.py:206
  259.4 79.1 %collective-permute-start.14 = (f32[1,1,2,16384]{3,1,2,0:T(1,128)S(1)}, f32[1,1,2,16384]{3,1,2,0:T(1,128)S(1)}, u32[]{:S(2)}, u32[]{:S(2)}) collective-permute-start(f32[1,1,2,16384]{3,1,2,0:T(1,128)S(1)} %get-tuple-element.112), channel_id=1, source_target_pairs={{0,1},{1,2},{2,3},{3,4},{4,5},{5,6},{6,7},{7,8},{8,9},{9,10},{10,1... | collective-permute-start | bytes 393224 | tf_op jit(solution)/shard_map/ppermute | solution.py:206
  260.4 78.1 %collective-permute-start.13 = (f32[1,1,2,16384]{3,1,2,0:T(1,128)S(1)}, f32[1,1,2,16384]{3,1,2,0:T(1,128)S(1)}, u32[]{:S(2)}, u32[]{:S(2)}) collective-permute-start(f32[1,1,2,16384]{3,1,2,0:T(1,128)S(1)} %get-tuple-element.113), channel_id=1, source_target_pairs={{0,2},{1,3},{2,4},{3,5},{4,6},{5,7},{6,8},{7,9},{8,10},{9,11},{10,... | collective-permute-start | bytes 393224 | tf_op jit(solution)/shard_map/ppermute | solution.py:206
  262.3 76.2 %collective-permute-start.12 = (f32[1,1,2,16384]{3,1,2,0:T(1,128)S(1)}, f32[1,1,2,16384]{3,1,2,0:T(1,128)S(1)}, u32[]{:S(2)}, u32[]{:S(2)}) collective-permute-start(f32[1,1,2,16384]{3,1,2,0:T(1,128)S(1)} %get-tuple-element.114), channel_id=1, source_target_pairs={{0,3},{1,4},{2,5},{3,6},{4,7},{5,8},{6,9},{7,10},{8,11},{9,12},{10... | collective-permute-start | bytes 393224 | tf_op jit(solution)/shard_map/ppermute | solution.py:206
  262.4 76.0 %collective-permute-start.11 = (f32[1,1,2,16384]{3,1,2,0:T(1,128)S(1)}, f32[1,1,2,16384]{3,1,2,0:T(1,128)S(1)}, u32[]{:S(2)}, u32[]{:S(2)}) collective-permute-start(f32[1,1,2,16384]{3,1,2,0:T(1,128)S(1)} %get-tuple-element.115), channel_id=1, source_target_pairs={{0,4},{1,5},{2,6},{3,7},{4,8},{5,9},{6,10},{7,11},{8,12},{9,13},{1... | collective-permute-start | bytes 393224 | tf_op jit(solution)/shard_map/ppermute | solution.py:206
  263.7 8.8 %collective-permute-start.1 = (f32[1,1,2,16384]{3,1,2,0:T(1,128)}, f32[1,1,2,16384]{3,1,2,0:T(1,128)S(1)}, u32[]{:S(2)}, u32[]{:S(2)}) collective-permute-start(f32[1,1,2,16384]{3,1,2,0:T(1,128)} %get-tuple-element.125), channel_id=1, source_target_pairs={{0,14},{1,15},{2,0},{3,1},{4,2},{5,3},{6,4},{7,5},{8,6},{9,7},{10,... | collective-permute-start | bytes 393224 | tf_op jit(solution)/shard_map/ppermute | solution.py:206
  272.5 7.0 %collective-permute-start.2 = (f32[1,1,2,16384]{3,1,2,0:T(1,128)}, f32[1,1,2,16384]{3,1,2,0:T(1,128)S(1)}, u32[]{:S(2)}, u32[]{:S(2)}) collective-permute-start(f32[1,1,2,16384]{3,1,2,0:T(1,128)} %get-tuple-element.124), channel_id=1, source_target_pairs={{0,13},{1,14},{2,15},{3,0},{4,1},{5,2},{6,3},{7,4},{8,5},{9,6},{10... | collective-permute-start | bytes 393224 | tf_op jit(solution)/shard_map/ppermute | solution.py:206
  279.5 5.1 collective-permute-start.3
  284.6 6.1 %collective-permute-start.4 = (f32[1,1,2,16384]{3,1,2,0:T(1,128)S(1)}, f32[1,1,2,16384]{3,1,2,0:T(1,128)S(1)}, u32[]{:S(2)}, u32[]{:S(2)}) collective-permute-start(f32[1,1,2,16384]{3,1,2,0:T(1,128)S(1)} %get-tuple-element.122), channel_id=1, source_target_pairs={{0,11},{1,12},{2,13},{3,14},{4,15},{5,0},{6,1},{7,2},{8,3},{9,4},{... | collective-permute-start | bytes 393224 | tf_op jit(solution)/shard_map/ppermute | solution.py:206
  290.7 6.1 %collective-permute-start.5 = (f32[1,1,2,16384]{3,1,2,0:T(1,128)S(1)}, f32[1,1,2,16384]{3,1,2,0:T(1,128)S(1)}, u32[]{:S(2)}, u32[]{:S(2)}) collective-permute-start(f32[1,1,2,16384]{3,1,2,0:T(1,128)S(1)} %get-tuple-element.121), channel_id=1, source_target_pairs={{0,10},{1,11},{2,12},{3,13},{4,14},{5,15},{6,0},{7,1},{8,2},{9,3},... | collective-permute-start | bytes 393224 | tf_op jit(solution)/shard_map/ppermute | solution.py:206
  296.8 10.5 %collective-permute-start.6 = (f32[1,1,2,16384]{3,1,2,0:T(1,128)S(1)}, f32[1,1,2,16384]{3,1,2,0:T(1,128)S(1)}, u32[]{:S(2)}, u32[]{:S(2)}) collective-permute-start(f32[1,1,2,16384]{3,1,2,0:T(1,128)S(1)} %get-tuple-element.120), channel_id=1, source_target_pairs={{0,9},{1,10},{2,11},{3,12},{4,13},{5,14},{6,15},{7,0},{8,1},{9,2},... | collective-permute-start | bytes 393224 | tf_op jit(solution)/shard_map/ppermute | solution.py:206
  307.3 7.5 %collective-permute-start.7 = (f32[1,1,2,16384]{3,1,2,0:T(1,128)S(1)}, f32[1,1,2,16384]{3,1,2,0:T(1,128)S(1)}, u32[]{:S(2)}, u32[]{:S(2)}) collective-permute-start(f32[1,1,2,16384]{3,1,2,0:T(1,128)S(1)} %get-tuple-element.119), channel_id=1, source_target_pairs={{0,8},{1,9},{2,10},{3,11},{4,12},{5,13},{6,14},{7,15},{8,0},{9,1},... | collective-permute-start | bytes 393224 | tf_op jit(solution)/shard_map/ppermute | solution.py:206
  314.8 9.7 %collective-permute-start.8 = (f32[1,1,2,16384]{3,1,2,0:T(1,128)S(1)}, f32[1,1,2,16384]{3,1,2,0:T(1,128)S(1)}, u32[]{:S(2)}, u32[]{:S(2)}) collective-permute-start(f32[1,1,2,16384]{3,1,2,0:T(1,128)S(1)} %get-tuple-element.118), channel_id=1, source_target_pairs={{0,7},{1,8},{2,9},{3,10},{4,11},{5,12},{6,13},{7,14},{8,15},{9,0},... | collective-permute-start | bytes 393224 | tf_op jit(solution)/shard_map/ppermute | solution.py:206
  324.5 7.1 %collective-permute-start.9 = (f32[1,1,2,16384]{3,1,2,0:T(1,128)S(1)}, f32[1,1,2,16384]{3,1,2,0:T(1,128)S(1)}, u32[]{:S(2)}, u32[]{:S(2)}) collective-permute-start(f32[1,1,2,16384]{3,1,2,0:T(1,128)S(1)} %get-tuple-element.117), channel_id=1, source_target_pairs={{0,6},{1,7},{2,8},{3,9},{4,10},{5,11},{6,12},{7,13},{8,14},{9,15},... | collective-permute-start | bytes 393224 | tf_op jit(solution)/shard_map/ppermute | solution.py:206
  331.6 6.8 %collective-permute-start.10 = (f32[1,1,2,16384]{3,1,2,0:T(1,128)S(1)}, f32[1,1,2,16384]{3,1,2,0:T(1,128)S(1)}, u32[]{:S(2)}, u32[]{:S(2)}) collective-permute-start(f32[1,1,2,16384]{3,1,2,0:T(1,128)S(1)} %get-tuple-element.116), channel_id=1, source_target_pairs={{0,5},{1,6},{2,7},{3,8},{4,9},{5,10},{6,11},{7,12},{8,13},{9,14},{... | collective-permute-start | bytes 393224 | tf_op jit(solution)/shard_map/ppermute | solution.py:206
  357.3 1.5 copy-start.11
  357.3 1.5 copy-start.12
  357.3 1.5 copy-start.16
  357.3 1.5 copy-start.17
  358.8 1.4 copy-start.13
  358.8 1.4 copy-start.19
  368.9 1.4 copy-start.10
  521.5 5.1 copy-start.5
  524.1 3.7 copy-start.6
  524.1 3.7 copy-start.7
  527.7 1.5 copy-start.8
  527.7 2.3 copy-start.9
Sparse Core Ops, SparseCore 0:
  162.8 34.4 all-gather.2
  199.4 33.0 all-gather.4
